TPU v7x, 32 devices: a whole 2x2x4 slice. The times are simulated.
32 devices in a mesh: wide: 16 (over z, y, x), narrow: 2 (over core).
Axes of the slice: x: 2, y: 2, z: 4, core: 2. Of those that a mesh axis runs over, the one named last changes fastest.
Arguments:
- tokens: bfloat16 [4096, 4096], P(('wide', 'narrow')), may hold values from -6 to 6
- expert_ids: int32 [4096, 2], P(('wide', 'narrow')), may hold values from 0 to 31, all different within a row; in each aligned block of 128 rows (0 to 127, 128 to 255, ...) at most 12 rows name the same one
- gate_values: bfloat16 [4096, 2], P(('wide', 'narrow')), may hold values from 0.099609375 to 1
- capacity: int32 [32], replicated, may hold values from 128 to 383
- w_gate: bfloat16 [32, 4096, 768], P(('wide', 'narrow')), may hold values from -0.09375 to 0.09375
- w_up: bfloat16 [32, 4096, 768], P(('wide', 'narrow')), may hold values from -0.09375 to 0.09375
- w_down: bfloat16 [32, 768, 4096], P(('wide', 'narrow')), may hold values from -0.21875 to 0.21875
Outputs:
- mixed: bfloat16 [4096, 4096], P(('wide', 'narrow'))
Inputs may be any that keep to these rules, and one draw needn't show every extreme that they name: `expert_ids`: the two experts of a token differ; among the tokens of one device no expert is named more than 12 times, and that many is reached.
All inputs are finite; a program needn't handle non-finite values.
Results may differ from a plain program's by a relative error of at most 0.0058.
Values may be sent and summed in bfloat16 or wider, within the bound.
A program may use at most 128 MiB of HBM per device.

v0:
```python
import jax
import jax.numpy as jnp
from jax import lax
from jax.sharding import PartitionSpec as P


def carried_in(value, axis, combine, identity):
    length, index = (lax.axis_size(axis), lax.axis_index(axis))
    everything = lax.all_gather(value, axis)
    start = jnp.broadcast_to(jnp.asarray(identity, value.dtype), value.shape)

    def hop(k, before):
        reached = k < index
        new = combine(before, everything[k])
        return jnp.where(reached, new, before)

    return lax.fori_loop(0, length, hop, start)


def expert_apply(token_rows, gate_matrix, up_matrix, down_matrix):
    gate_part = jnp.dot(token_rows, gate_matrix, preferred_element_type=jnp.float32)
    up_part = jnp.dot(token_rows, up_matrix, preferred_element_type=jnp.float32)
    hidden = (jax.nn.silu(gate_part) * up_part).astype(jnp.bfloat16)
    return jnp.dot(hidden, down_matrix, preferred_element_type=jnp.float32).astype(jnp.bfloat16)


def add_counts(earlier, later):
    return earlier + later


def on_device(tokens, expert_ids, gate_values, capacity, w_gate, w_up, w_down):
    experts = capacity.shape[0]
    tok_rows = tokens.shape[0]
    width = tokens.shape[1]
    most_rows = 3 * tok_rows // experts
    flat_ids = expert_ids.reshape(-1)
    onehot = (flat_ids[:, None] == jnp.arange(experts, dtype=jnp.int32)[None, :]).astype(jnp.int32)
    local_counts = jnp.sum(onehot, axis=0)
    earlier_counts = carried_in(
        local_counts, ("wide", "narrow"), add_counts, jnp.zeros((experts,), jnp.int32)
    )
    local_rank = jnp.sum((jnp.cumsum(onehot, axis=0) - onehot) * onehot, axis=1)
    global_rank = local_rank + jnp.sum(onehot * earlier_counts[None, :], axis=1)
    limit = jnp.sum(onehot * capacity[None, :], axis=1)
    kept_mask = global_rank < limit
    slot_index = flat_ids * most_rows + local_rank
    token_rows = jnp.repeat(tokens, 2, axis=0)
    token_rows = jnp.where(kept_mask[:, None], token_rows, jnp.zeros_like(token_rows))
    outgoing = jnp.zeros((experts * most_rows, width), jnp.bfloat16).at[slot_index].set(token_rows)
    gate_matrix = w_gate[0]
    up_matrix = w_up[0]
    down_matrix = w_down[0]
    outgoing = outgoing.reshape(experts, most_rows, width)
    arrived = lax.all_to_all(outgoing, ("wide", "narrow"), split_axis=0, concat_axis=0, tiled=True)
    count_items = arrived.shape[1]
    results = expert_apply(arrived.reshape(-1, width), gate_matrix, up_matrix, down_matrix)
    results = results.reshape(experts, count_items, width)
    answers = lax.all_to_all(results, ("wide", "narrow"), split_axis=0, concat_axis=0, tiled=True)
    answers = answers.reshape(experts * most_rows, width)
    picked = answers[slot_index]
    weights = gate_values.reshape(-1).astype(jnp.float32) * kept_mask.astype(jnp.float32)
    scaled = picked.astype(jnp.float32) * weights[:, None]
    mixed = jnp.sum(scaled.reshape(tok_rows, 2, width), axis=1)
    return mixed.astype(jnp.bfloat16)


def solution(mesh):
    return jax.shard_map(
        on_device,
        mesh=mesh,
        in_specs=(
            P(("wide", "narrow"), None),
            P(("wide", "narrow"), None),
            P(("wide", "narrow"), None),
            P(),
            P(("wide", "narrow"), None, None),
            P(("wide", "narrow"), None, None),
            P(("wide", "narrow"), None, None),
        ),
        out_specs=P(("wide", "narrow"), None),
        check_vma=False,
    )
```

profile of v0, /device:TPU:0, one launch (start us, length us, event | category | flops | bytes accessed | tf_op | source)
XLA Modules:
  0.0 307.8 jit_solution(10622250146650895442)
XLA Ops:
  0.0 0.8 copy.10
  0.8 0.1 eq.25
  0.9 0.1 eq.29
  1.1 0.7 broadcast_multiply_fusion
  1.8 0.1 convert_reduce_fusion
  1.9 0.2 dynamic-update-slice
  2.1 42.0 %all-reduce = s32[1024]{0:T(1024)S(1)} all-reduce(s32[1024]{0:T(1024)S(1)} %dynamic-update-slice), channel_id=2, replica_groups=mesh['wide'=16,'narrow'=2] {'wide','narrow'}, use_global_device_ids=true, to_apply=%add | all-reduce | flops 1024 | bytes 8192
  44.1 0.1 reshape.120
  44.2 1.3 while.14
  45.5 0.6 reduce-window.6
  46.1 0.2 slice_reduce_fusion
  46.3 0.1 copy.9
  46.4 0.1 mul.59
  46.5 0.0 copy-start
  46.6 3.3 %broadcast_in_dim.30 = bf16[128,2,4096]{2,1,0:T(2,128)(2,1)S(1)} broadcast(bf16[128,4096]{1,0:T(8,128)(2,1)} %param.9), dimensions={0,2} | broadcast | bytes 3145728 | tf_op jit(solution)/shard_map/broadcast_in_dim | solution.py:47
  49.9 2.2 reshape.98
  52.1 0.0 copy-done
  52.1 0.1 select_reduce_fusion.1
  52.3 5.6 %scatter_custom_fusion = bf16[384,4096]{1,0:T(8,128)(2,1)S(1)} fusion(s32[256]{0:T(256)S(1)} %bitcast.37, bf16[256,4096]{1,0:T(8,128)(2,1)} %reshape.98, pred[256]{0:T(512)(128)(4,1)S(1)} %add_compare_fusion, bf16[]{:T(256)} %constant.46.clone.1), kind=kCustom, calls=%fused_computation.12 | custom fusion | flops 1048576 | bytes 5244416 | tf_op jit(solution)/shard_map/scatter | solution.py:49
  57.8 2.7 reshape.99
  60.5 98.1 %all_to_all.10 = bf16[32,12,4096]{2,1,0:T(8,128)(2,1)} all-to-all(bf16[32,12,4096]{2,1,0:T(8,128)(2,1)} %reshape.99), channel_id=1, replica_groups=mesh['wide'=16,'narrow'=2] {'wide','narrow'}, dimensions={0} | all-to-all | bytes 6291456 | tf_op jit(solution)/shard_map/all_to_all | solution.py:54
  158.7 4.0 %reshape.100 = bf16[384,4096]{1,0:T(8,128)(2,1)S(1)} reshape(bf16[32,12,4096]{2,1,0:T(8,128)(2,1)} %all_to_all.10) | data formatting | bytes 6291456 | tf_op jit(solution)/shard_map/reshape | solution.py:56
  162.6 6.4 %fusion.4 = f32[384,768]{1,0:T(8,128)} fusion(bf16[384,4096]{1,0:T(8,128)(2,1)S(1)} %reshape.100, bf16[1,4096,768]{2,1,0:T(8,128)(2,1)} %param.13), kind=kOutput, calls=%fused_computation.8 | convolution fusion | flops 2415919104 | bytes 10616832 | tf_op jit(solution)/shard_map/dot_general | solution.py:21
  169.0 13.3 %fusion.6 = bf16[384,4096]{1,0:T(8,128)(2,1)} fusion(bf16[1,768,4096]{2,1,0:T(8,128)(2,1)} %param.15, bf16[384,4096]{1,0:T(8,128)(2,1)S(1)} %reshape.100, bf16[1,4096,768]{2,1,0:T(8,128)(2,1)} %param.14, f32[384,768]{1,0:T(8,128)} %fusion.4), kind=kOutput, calls=%fused_computation.10 | convolution fusion | flops 4835180544 | bytes 20054016 | tf_op jit(solution)/shard_map/dot_general | solution.py:24
  182.3 5.5 %reshape.101 = bf16[32,12,4096]{2,1,0:T(8,128)(2,1)} reshape(bf16[384,4096]{1,0:T(8,128)(2,1)} %fusion.6) | data formatting | bytes 6291456 | tf_op jit(solution)/shard_map/reshape | solution.py:57
  187.8 0.0 copy-start.1
  187.8 4.0 %all-to-all-start.1 = ((bf16[32,12,4096]{2,1,0:T(8,128)(2,1)}), bf16[32,12,4096]{2,1,0:T(8,128)(2,1)}, u32[]{:S(2)}, u32[]{:S(2)}) async-start(bf16[32,12,4096]{2,1,0:T(8,128)(2,1)} %reshape.101), calls=%async_computation.1 | async-start | bytes 8388608 | tf_op jit(solution)/shard_map/all_to_all | solution.py:58
  191.9 0.2 lt.43
  192.0 0.0 copy-done.1
  192.0 0.1 copy.13
  192.2 93.4 %all-to-all-done.1 = bf16[32,12,4096]{2,1,0:T(8,128)(2,1)} async-done(((bf16[32,12,4096]{2,1,0:T(8,128)(2,1)}), bf16[32,12,4096]{2,1,0:T(8,128)(2,1)}, u32[]{:S(2)}, u32[]{:S(2)}) %all-to-all-start.1) | async-done | bytes 3145760 | tf_op jit(solution)/shard_map/all_to_all | solution.py:58
  285.5 4.0 %reshape.102 = bf16[384,4096]{1,0:T(8,128)(2,1)S(1)} reshape(bf16[32,12,4096]{2,1,0:T(8,128)(2,1)} %all-to-all-done.1) | data formatting | bytes 6291456 | tf_op jit(solution)/shard_map/reshape | solution.py:59
  289.5 3.2 %gather_fusion = bf16[256,4096]{1,0:T(8,128)(2,1)} fusion(bf16[384,4096]{1,0:T(8,128)(2,1)S(1)} %reshape.102, s32[1024]{0:T(1024)S(1)} %pad_clamp_fusion), kind=kCustom, calls=%fused_computation | custom fusion | bytes 4195328 | tf_op jit(solution)/shard_map/gather | solution.py:60
  292.7 5.4 %reshape.103 = f32[128,2,4096]{2,1,0:T(2,128)} reshape(bf16[256,4096]{1,0:T(8,128)(2,1)} %gather_fusion) | data formatting | bytes 6291456 | tf_op jit(solution)/shard_map/convert_element_type | solution.py:62
  298.1 9.6 %multiply_reduce_fusion = bf16[128,4096]{1,0:T(8,128)(2,1)} fusion(f32[128,2,4096]{2,1,0:T(2,128)} %reshape.103, f32[128,2]{1,0:T(8,128)S(1)} %broadcast_select_fusion.2), kind=kLoop, calls=%fused_computation.11 | loop fusion | flops 1572864 | bytes 5243904 | tf_op jit(solution)/shard_map/reduce_sum | solution.py:63
  (41 shorter events, 0.6 us)
Async XLA Ops:
  46.5 5.6 %copy-start = (s32[32]{0:T(128)S(1)}, s32[32]{0:T(128)}, u32[]{:S(2)}) copy-start(s32[32]{0:T(128)} %param.12) | copy-start | bytes 388
  187.8 4.2 %copy-start.1 = (bf16[128,2]{0,1:T(2,128)(2,1)S(1)}, bf16[128,2]{0,1:T(2,128)(2,1)}, u32[]{:S(2)}) copy-start(bf16[128,2]{0,1:T(2,128)(2,1)} %param.11) | copy-start | bytes 1540
  187.8 97.7 %all-to-all-start.1 = ((bf16[32,12,4096]{2,1,0:T(8,128)(2,1)}), bf16[32,12,4096]{2,1,0:T(8,128)(2,1)}, u32[]{:S(2)}, u32[]{:S(2)}) async-start(bf16[32,12,4096]{2,1,0:T(8,128)(2,1)} %reshape.101), calls=%async_computation.1 | async-start | bytes 8388608 | tf_op jit(solution)/shard_map/all_to_all | solution.py:58
where the time goes:
time: 309 us; the launch traced here: 308 us
  blocking collectives  140 us (45%)
  waiting for transfers between devices  93.4 us (30%)
  local copies, waits for them, and re-layouts  32.4 us (10%)
  matrix products  19.7 us (6%)
  other arithmetic  17.3 us (6%)
  starting transfers between devices  4.01 us (1%)
    all_to_all x1, blocking collectives, on_device(): lax.all_to_all(outgoing, ('wide', 'narrow'), split_axis=0, concat_axis=0,...  98.1 us
    all_to_all x1, waiting for transfers between devices, on_device(): lax.all_to_all(results, ('wide', 'narrow'), split_axis=0, concat_axis=0,...  93.4 us
    unnamed x1, blocking collectives  42 us
    dot_general x1, matrix products, expert_apply(): jnp.dot(hidden, down_matrix, preferred_element_type=jnp.float32)  13.3 us
    reduce_sum x1, other arithmetic, on_device(): mixed = jnp.sum(scaled.reshape(tok_rows, 2, width), axis=1)  9.64 us
    dot_general x1, matrix products, expert_apply(): jnp.dot(token_rows, gate_matrix, preferred_element_type=jnp.float32)  6.39 us
  transfers between devices with their start and end apart: 1, of which 1 were waited for; matrix products, arithmetic and copies ran while one was open for 0% of the time, Pallas kernels for 0%

commit v1 on v0

v1 whole, which is shorter than its diff:
```python
import functools
import math

import jax
import jax.numpy as jnp
import numpy as np
from jax import lax
from jax.experimental import pallas as pl
from jax.experimental.pallas import tpu as pltpu
from jax.sharding import PartitionSpec as P

MESH = pl.DeviceIdType.MESH
PIECES = 16
F32 = jnp.float32
BF16 = jnp.bfloat16


def flip(me, off, bits):
    out = 0
    for b in range(bits):
        w = 1 << b
        out = out + (((me // w) % 2 + (off // w) % 2) % 2) * w
    return out


def alternate(k, groups):
    return (k % 2) * (groups - 1 - k // 2) + (1 - k % 2) * (k // 2)


def kernel(n, narrow, most, unit, tok, put, mix, pick, counts, cap, rank, row_mask, col_mask, gather, spread,
           wg_hbm, wu_hbm, wd_hbm, out,
           wg, wu, wd, sent, came, back, home, x, y, total, seen,
           s1, r1, s2, r2, s3, r3, wsem):
    bits = int(math.log2(n))
    groups = n // unit
    rows = unit * unit * most
    part = unit * most
    width = tok.shape[1]
    piece = width // PIECES
    quads = PIECES // unit
    me = lax.axis_index("wide") * narrow + lax.axis_index("narrow")

    def where_is(off):
        peer = flip(me, off, bits)
        return (peer // narrow, peer % narrow)

    loads = [
        pltpu.make_async_copy(h.at[0], v, wsem.at[i])
        for i, (h, v) in enumerate(((wg_hbm, wg), (wu_hbm, wu), (wd_hbm, wd)))
    ]
    for load in loads:
        load.start()

    barrier = pltpu.get_barrier_semaphore()

    @pl.loop(1, n)
    def _(off):
        pl.semaphore_signal(barrier, inc=1, device_id=where_is(off), device_id_type=MESH)

    pl.semaphore_wait(barrier, n - 1)

    def count_copy(off):
        return pltpu.make_async_remote_copy(
            src_ref=counts, dst_ref=seen.at[off], send_sem=s3.at[off], recv_sem=r3.at[off],
            device_id=where_is(off), device_id_type=MESH)

    def out_copy(off):
        return pltpu.make_async_remote_copy(
            src_ref=sent.at[off], dst_ref=came.at[off], send_sem=s1.at[off], recv_sem=r1.at[off],
            device_id=where_is(off), device_id_type=MESH)

    def back_copy(off):
        return pltpu.make_async_remote_copy(
            src_ref=back.at[off], dst_ref=home.at[off], send_sem=s2.at[off], recv_sem=r2.at[off],
            device_id=where_is(off), device_id_type=MESH)

    def each_remote(g, act):
        for i in range(unit):
            off = g * unit + i
            if i:
                act(off)
            else:
                @pl.when(g > 0)
                def _(off=off):
                    act(off)

    @pl.loop(0, groups)
    def _(k):
        g = (groups - 1) * ((k + 1) % 2) - (k // 2) * ((k + 1) % 2) + (k // 2) * (k % 2)
        onehot = put[g]
        masked = [onehot * row_mask[j] for j in range(unit)]
        for q in range(quads):
            acc = jnp.zeros((rows, piece), F32)
            for j in range(unit):
                at = (q * unit + j) * piece
                acc = acc + jnp.dot(masked[j], tok[:, at:at + piece], preferred_element_type=F32)
            block = acc.astype(BF16).reshape(unit, part, piece)
            sent[pl.ds(g * unit, unit), q * part:(q + 1) * part, :] = block
        each_remote(g, lambda off: out_copy(off).start())

        @pl.when(g == 0)
        def _():
            came[0] = sent[0]

    @pl.loop(1, n)
    def _(off):
        count_copy(off).start()

    for load in loads:
        load.wait()

    @pl.loop(0, groups)
    def _(k):
        g = alternate(k, groups)
        each_remote(g, lambda off: out_copy(off).wait_recv())
        for q in range(quads):
            block = came[pl.ds(g * unit, unit), q * part:(q + 1) * part, :].reshape(rows, piece)
            for j in range(unit):
                at = (q * unit + j) * piece
                x[:, at:at + piece] = jnp.dot(gather[j], block, preferred_element_type=F32).astype(BF16)
        xs = x[...]
        gate = jnp.dot(xs, wg[...], preferred_element_type=F32)
        up = jnp.dot(xs, wu[...], preferred_element_type=F32)
        hidden = (gate / (1.0 + jnp.exp(-gate)) * up).astype(BF16)
        y[...] = jnp.dot(hidden, wd[...], preferred_element_type=F32).astype(BF16)
        for q in range(quads):
            acc = jnp.zeros((rows, piece), F32)
            for j in range(unit):
                at = (q * unit + j) * piece
                acc = acc + jnp.dot(spread[j], y[:, at:at + piece], preferred_element_type=F32)
            block = acc.astype(BF16).reshape(unit, part, piece)
            back[pl.ds(g * unit, unit), q * part:(q + 1) * part, :] = block
        each_remote(g, lambda off: back_copy(off).start())

        @pl.when(g == 0)
        def _():
            home[0] = back[0]

    seen[0] = jnp.zeros_like(seen[0])

    @pl.loop(1, n)
    def _(off):
        count_copy(off).wait()

    def earlier(off, tally):
        ahead = jnp.where(flip(me, off, bits) < me, 1, 0)
        return tally + seen[off] * ahead

    before = lax.fori_loop(1, n, earlier, jnp.zeros(counts.shape, jnp.int32))
    left = jnp.clip(cap[...] - before, 0, most).astype(F32).astype(BF16)

    total[...] = jnp.zeros_like(total)

    @pl.loop(0, groups)
    def _(k):
        g = alternate(k, groups)
        room = jnp.dot(left, pick[g], preferred_element_type=F32)[0:1, :]
        kept = jnp.where(room > rank[...], 1.0, 0.0).astype(BF16)
        weights = mix[g] * kept
        masked = [weights * col_mask[j] for j in range(unit)]
        each_remote(g, lambda off: back_copy(off).wait_recv())
        for q in range(quads):
            block = home[pl.ds(g * unit, unit), q * part:(q + 1) * part, :].reshape(rows, piece)
            for j in range(unit):
                at = (q * unit + j) * piece
                total[:, at:at + piece] += jnp.dot(masked[j], block, preferred_element_type=F32)

    out[...] = total[...].astype(BF16)

    @pl.loop(1, n)
    def _(off):
        out_copy(off).wait_send()
        back_copy(off).wait_send()


def on_device(n, narrow, tokens, expert_ids, gate_values, capacity, w_gate, w_up, w_down):
    experts = capacity.shape[0]
    tok_rows, width = tokens.shape
    hidden = w_gate.shape[2]
    most = 3 * tok_rows // experts
    unit = 16 // math.gcd(16, most)
    groups = n // unit
    rows = unit * unit * most
    me = lax.axis_index("wide") * narrow + lax.axis_index("narrow")
    me = me.astype(jnp.int32)

    flat = expert_ids.reshape(-1)
    onehot = (flat[:, None] == jnp.arange(experts, dtype=jnp.int32)[None, :]).astype(BF16)
    triangle = jnp.asarray(np.tril(np.ones((2 * tok_rows,) * 2), -1), BF16)
    before = jnp.dot(triangle, onehot, preferred_element_type=F32)
    rank = jnp.sum(before * onehot.astype(F32), axis=1).astype(jnp.int32)
    tally = jnp.sum(onehot.astype(F32), axis=0).astype(jnp.int32)
    lanes = -(-experts // 128) * 128
    counts = jnp.broadcast_to(jnp.pad(tally, (0, lanes - experts))[None], (8, lanes))
    cap = jnp.broadcast_to(jnp.pad(capacity, (0, lanes - experts))[None], (8, lanes))
    slot = ((flat ^ me) * most + rank).reshape(tok_rows, 2)

    i, j, r = np.meshgrid(np.arange(unit), np.arange(unit), np.arange(most), indexing="ij")
    i, j, r = i.reshape(-1), j.reshape(-1), r.reshape(-1)
    code = (np.arange(groups)[:, None] * unit + i[None]) * most + r[None]
    partner = np.arange(groups)[:, None] * unit + i[None]
    code, partner = jnp.asarray(code, jnp.int32), jnp.asarray(partner, jnp.int32)
    hit = [slot[:, c][None, :] == code[:, :, None] for c in (0, 1)]
    put = (hit[0] | hit[1]).astype(BF16)
    mix = sum(
        jnp.where(slot[:, c][None, :, None] == code[:, None, :], gate_values[:, c][None, :, None], 0)
        for c in (0, 1)
    ).astype(BF16)
    pick = (jnp.arange(lanes, dtype=jnp.int32)[None, :, None] == (partner ^ me)[:, None, :]).astype(BF16)
    rank_row = jnp.asarray(r[None], F32)
    which = np.arange(unit)
    row_mask = jnp.asarray(np.broadcast_to((j[None] == which[:, None])[:, :, None], (unit, rows, tok_rows)), BF16)
    col_mask = jnp.asarray((j[None] == which[:, None])[:, None, :], BF16)
    short = np.arange(unit * most)
    gather = (short[None, :, None] == (i * most + r)[None, None, :]) & (j[None] == which[:, None])[:, None, :]
    gather, spread = jnp.asarray(gather, BF16), jnp.asarray(gather.transpose(0, 2, 1), BF16)

    block = (PIECES * most, width // PIECES)
    vmem = pl.BlockSpec(memory_space=pltpu.VMEM)
    hbm = pl.BlockSpec(memory_space=pl.ANY)
    dma = pltpu.SemaphoreType.DMA
    return pl.pallas_call(
        functools.partial(kernel, n, narrow, most, unit),
        out_shape=jax.ShapeDtypeStruct((tok_rows, width), BF16),
        in_specs=[vmem] * 11 + [hbm] * 3,
        out_specs=vmem,
        scratch_shapes=[
            pltpu.VMEM((width, hidden), BF16),
            pltpu.VMEM((width, hidden), BF16),
            pltpu.VMEM((hidden, width), BF16),
            pltpu.VMEM((n,) + block, BF16),
            pltpu.VMEM((n,) + block, BF16),
            pltpu.VMEM((n,) + block, BF16),
            pltpu.VMEM((n,) + block, BF16),
            pltpu.VMEM((unit * most, width), BF16),
            pltpu.VMEM((unit * most, width), BF16),
            pltpu.VMEM((tok_rows, width), F32),
            pltpu.VMEM((n, 8, lanes), jnp.int32),
            dma((n,)), dma((n,)), dma((n,)), dma((n,)), dma((n,)), dma((n,)), dma((3,)),
        ],
        compiler_params=pltpu.CompilerParams(
            collective_id=0, has_side_effects=True, vmem_limit_bytes=60 * 1024 * 1024
        ),
    )(tokens, put, mix, pick, counts, cap, rank_row, row_mask, col_mask, gather, spread, w_gate, w_up, w_down)


def solution(mesh):
    both = ("wide", "narrow")
    n, narrow = mesh.shape["wide"] * mesh.shape["narrow"], mesh.shape["narrow"]
    return jax.shard_map(
        functools.partial(on_device, n, narrow),
        mesh=mesh,
        in_specs=(P(both, None), P(both, None), P(both, None), P(),
                  P(both, None, None), P(both, None, None), P(both, None, None)),
        out_specs=P(both, None),
        check_vma=False,
    )
```

time: 309 us -> 173 us (0.56)
  Pallas kernels: 0 us -> 160 us
  blocking collectives: 140 us -> 0 us
  waiting for transfers between devices: 93.4 us -> 0 us
  local copies, waits for them, and re-layouts: 32.4 us -> 6.09 us
  matrix products: 19.7 us -> 1.11 us
  other arithmetic: 17.3 us -> 5.34 us
  starting transfers between devices: 4.01 us -> 0 us
    pallas_call x0 -> x1, Pallas kernels: none -> 160 us  [on_device(): pl.pallas_call(functools.partial(kernel, n, narrow, most, unit), out_shap...]
    all_to_all x1 -> x0, blocking collectives: 98.1 us -> none  [on_device(): lax.all_to_all(outgoing, ('wide', 'narrow'), split_axis=0, concat_axis=0,...]
    all_to_all x1 -> x0, waiting for transfers between devices: 93.4 us -> none  [on_device(): lax.all_to_all(results, ('wide', 'narrow'), split_axis=0, concat_axis=0,...]
    unnamed x1 -> x0, blocking collectives: 42 us -> none
    dot_general x2 -> x1, matrix products: 19.7 us -> 1.11 us  [on_device(): before = jnp.dot(triangle, onehot, preferred_element_type=F32)]
    reshape x5 -> x0, local copies, waits for them, and re-layouts: 18.4 us -> none  [the longest x1 5.5 us: on_device(): results = results.reshape(experts, count_items, width)]
    reduce_sum x3 -> x1, other arithmetic: 9.84 us -> 0.11 us  [on_device(): tally = jnp.sum(onehot.astype(F32), axis=0).astype(jnp.int32)]
    scatter x1 -> x0, other arithmetic: 5.56 us -> none  [on_device(): jnp.zeros((experts * most_rows, width), jnp.bfloat16).at[slot_index]]
  transfers between devices with their start and end apart: 1 -> 0, of which waited for: 1 -> 0; matrix products, arithmetic and copies ran while one was open for 0% -> 0% of each run, Pallas kernels for 0% -> 0%
where the time goes in v1:
time: 173 us
  Pallas kernels  160 us (92%)
  local copies, waits for them, and re-layouts  6.09 us (4%)
  other arithmetic  5.34 us (3%)
    pallas_call x1, Pallas kernels, on_device(): pl.pallas_call(functools.partial(kernel, n, narrow, most, unit), out_shap...  160 us

profile of v1, /device:TPU:0, one launch (start us, length us, event | category | flops | bytes accessed | tf_op | source)
XLA Modules:
  0.0 172.6 jit_solution(11353389297334678185)
XLA Ops:
  0.0 0.7 pad.8
  0.7 0.7 slice_bitcast_fusion.1
  1.4 0.6 broadcast_in_dim.47.cap
  2.0 0.7 broadcast_xor_fusion
  2.7 0.8 copy.18
  3.5 0.1 eq.38
  3.6 0.1 convert_reduce_fusion
  3.7 1.1 fusion
  4.9 0.6 broadcast_in_dim.46.counts
  5.5 0.1 convert_element_type.29
  5.6 0.2 slice_reduce_fusion.1
  5.8 1.7 or_convert_fusion.put
  7.5 1.0 fusion.1.pick
  8.5 1.8 %fusion.2.mix = bf16[8,128,192]{2,1,0:T(8,128)(2,1)} fusion(s32[8,192]{1,0:T(8,128)} %constant.35.clone, s32[128]{0:T(128)S(1)} %get-tuple-element.6, s32[128]{0:T(128)S(1)} %get-tuple-element.5, bf16[128]{0:T(256)(128)(2,1)S(1)} %get-tuple-element.8, bf16[128]{0:T(256)(128)(2,1)S(1)} %get-tuple-element.7), kind=kLoop, calls=%fused_computation.7 | loop fusion | flops 983040 | bytes 400896 | tf_op jit(solution)/shard_map/add | solution.py:205
  10.3 160.0 %shard_map.145 = bf16[128,4096]{1,0:T(8,128)(2,1)} custom-call(bf16[128,4096]{1,0:T(8,128)(2,1)} %tok.1, bf16[8,192,128]{2,1,0:T(8,128)(2,1)} %or_convert_fusion.put, bf16[8,128,192]{2,1,0:T(8,128)(2,1)} %fusion.2.mix, bf16[8,128,192]{2,1,0:T(8,128)(2,1)} %fusion.1.pick, s32[8,128]{1,0:T(8,128)} %broadcast_in_dim.46.counts, s32[8,128]{1,0:T(8,128)} %broadcast_in_dim.47.cap, ...), custom_call_target="tpu_custom_call" | custom-call | tf_op jit(solution)/shard_map/pallas_call | solution.py:222
  170.3 2.3 %copy.21 = bf16[128,4096]{1,0:T(8,128)(2,1)} copy(bf16[128,4096]{1,0:T(8,128)(2,1)} %shard_map.145) | data formatting | bytes 2097152
  (4 shorter events, 0.0 us)

commit v2 on v1

--- a/solution.py
+++ b/solution.py
@@ -23,8 +23,25 @@
     return out
 
 
-def alternate(k, groups):
-    return (k % 2) * (groups - 1 - k // 2) + (1 - k % 2) * (k // 2)
+def orders(groups):
+    if groups != 8:
+        return None
+    return [sum(g * 8**k for k, g in enumerate(o)) for o in ((7, 0, 1, 2, 6, 3, 5, 4), (0, 1, 7, 2, 6, 3, 5, 4))]
+
+
+def in_order(groups, which, body):
+    if orders(groups) is None:
+        def plain(k, carry):
+            body(k)
+            return carry
+        lax.fori_loop(0, groups, plain, 0)
+        return
+
+    def step(k, digits):
+        body(digits % groups)
+        return digits // groups
+
+    lax.fori_loop(0, groups, step, jnp.int32(orders(groups)[which]))
 
 
 def kernel(n, narrow, most, unit, tok, put, mix, pick, counts, cap, rank, row_mask, col_mask, gather, spread,
@@ -84,9 +101,7 @@
                 def _(off=off):
                     act(off)
 
-    @pl.loop(0, groups)
-    def _(k):
-        g = (groups - 1) * ((k + 1) % 2) - (k // 2) * ((k + 1) % 2) + (k // 2) * (k % 2)
+    def dispatch(g):
         onehot = put[g]
         masked = [onehot * row_mask[j] for j in range(unit)]
         for q in range(quads):
@@ -102,6 +117,8 @@
         def _():
             came[0] = sent[0]
 
+    in_order(groups, 0, dispatch)
+
     @pl.loop(1, n)
     def _(off):
         count_copy(off).start()
@@ -109,9 +126,7 @@
     for load in loads:
         load.wait()
 
-    @pl.loop(0, groups)
-    def _(k):
-        g = alternate(k, groups)
+    def expert(g):
         each_remote(g, lambda off: out_copy(off).wait_recv())
         for q in range(quads):
             block = came[pl.ds(g * unit, unit), q * part:(q + 1) * part, :].reshape(rows, piece)
@@ -136,6 +151,8 @@
         def _():
             home[0] = back[0]
 
+    in_order(groups, 1, expert)
+
     seen[0] = jnp.zeros_like(seen[0])
 
     @pl.loop(1, n)
@@ -151,9 +168,7 @@
 
     total[...] = jnp.zeros_like(total)
 
-    @pl.loop(0, groups)
-    def _(k):
-        g = alternate(k, groups)
+    def combine(g):
         room = jnp.dot(left, pick[g], preferred_element_type=F32)[0:1, :]
         kept = jnp.where(room > rank[...], 1.0, 0.0).astype(BF16)
         weights = mix[g] * kept
@@ -164,6 +179,8 @@
             for j in range(unit):
                 at = (q * unit + j) * piece
                 total[:, at:at + piece] += jnp.dot(masked[j], block, preferred_element_type=F32)
+
+    in_order(groups, 1, combine)
 
     out[...] = total[...].astype(BF16)
 

time: 173 us -> 172 us (level)
  no operation moved by 1% of the time
where the time goes in v2:
time: 172 us
  Pallas kernels  159 us (92%)
  local copies, waits for them, and re-layouts  6.09 us (4%)
  other arithmetic  5.34 us (3%)
    pallas_call x1, Pallas kernels, on_device(): pl.pallas_call(functools.partial(kernel, n, narrow, most, unit), out_shap...  159 us

profile of v2, /device:TPU:0, one launch (start us, length us, event | category | flops | bytes accessed | tf_op | source)
XLA Modules:
  0.0 171.6 jit_solution(2033492641383649990)
XLA Ops:
  0.0 0.7 pad.8
  0.7 0.7 slice_bitcast_fusion.1
  1.4 0.6 broadcast_in_dim.47.cap
  2.0 0.7 broadcast_xor_fusion
  2.7 0.8 copy.18
  3.5 0.1 eq.38
  3.6 0.1 convert_reduce_fusion
  3.7 1.1 fusion
  4.9 0.6 broadcast_in_dim.46.counts
  5.5 0.1 convert_element_type.29
  5.6 0.2 slice_reduce_fusion.1
  5.8 1.7 or_convert_fusion.put
  7.5 1.0 fusion.1.pick
  8.5 1.8 %fusion.2.mix = bf16[8,128,192]{2,1,0:T(8,128)(2,1)} fusion(s32[8,192]{1,0:T(8,128)} %constant.35.clone, s32[128]{0:T(128)S(1)} %get-tuple-element.6, s32[128]{0:T(128)S(1)} %get-tuple-element.5, bf16[128]{0:T(256)(128)(2,1)S(1)} %get-tuple-element.8, bf16[128]{0:T(256)(128)(2,1)S(1)} %get-tuple-element.7), kind=kLoop, calls=%fused_computation.7 | loop fusion | flops 983040 | bytes 400896 | tf_op jit(solution)/shard_map/add | solution.py:222
  10.3 159.0 %shard_map.145 = bf16[128,4096]{1,0:T(8,128)(2,1)} custom-call(bf16[128,4096]{1,0:T(8,128)(2,1)} %tok.1, bf16[8,192,128]{2,1,0:T(8,128)(2,1)} %or_convert_fusion.put, bf16[8,128,192]{2,1,0:T(8,128)(2,1)} %fusion.2.mix, bf16[8,128,192]{2,1,0:T(8,128)(2,1)} %fusion.1.pick, s32[8,128]{1,0:T(8,128)} %broadcast_in_dim.46.counts, s32[8,128]{1,0:T(8,128)} %broadcast_in_dim.47.cap, ...), custom_call_target="tpu_custom_call" | custom-call | tf_op jit(solution)/shard_map/pallas_call | solution.py:239
  169.4 2.3 %copy.21 = bf16[128,4096]{1,0:T(8,128)(2,1)} copy(bf16[128,4096]{1,0:T(8,128)(2,1)} %shard_map.145) | data formatting | bytes 2097152
  (4 shorter events, 0.0 us)
